TPU v7x, 512 devices: a whole 4x8x8 slice. The times are simulated.
512 devices in a mesh: cfg: 2 (over x_lo), ctx: 32 (over y, x_hi, core), tp: 8 (over z).
Axes of the slice: x: 4 (x_hi: 2, x_lo: 2; x = x_hi * 2 + x_lo), y: 8, z: 8, core: 2. Of those that a mesh axis runs over, the one named last changes fastest.
Arguments:
- query_proj: bfloat16 [2, 8192, 3072], P('cfg', 'ctx', 'tp'), may hold values from -8 to 8
- key_proj: bfloat16 [2, 8192, 3072], P('cfg', 'ctx', 'tp'), may hold values from -8 to 8
- value_proj: bfloat16 [2, 8192, 3072], P('cfg', 'ctx', 'tp'), may hold values from -6 to 6
- query_gain: float32 [128], replicated, may hold values from 1 to 8
- key_gain: float32 [128], replicated, may hold values from 1 to 8
- block_input: bfloat16 [2, 8192, 3072], P('cfg', ('ctx', 'tp')), may hold values from -120 to 120
- cached_out: bfloat16 [2, 8192, 3072], P('cfg', ('ctx', 'tp')), may hold values from -120 to 120
- replay_mask: int32 [2, 8192], P('cfg', 'ctx'), may hold values from 0 to 1, as said below
- branch_gate: float32 [2, 3072], P('cfg'), may hold values from 1 to 4
- attn_weight: bfloat16 [3072, 3072], P('tp'), may hold values from -0.109375 to 0.109375
- final_shift: float32 [2, 3072], P('cfg'), may hold values from -4 to 4
- final_scale: float32 [2, 3072], P('cfg'), may hold values from -2 to 2
- patch_weight: bfloat16 [3072, 64], replicated, may hold values from -0.109375 to 0.109375
Outputs:
- block_out: bfloat16 [2, 8192, 3072], P('cfg', ('ctx', 'tp'))
- velocity: float32 [8192, 64], P(('ctx', 'tp'), 'cfg')
Inputs may be any that keep to these rules, and one draw needn't show every extreme that they name: `replay_mask`: in each branch, at most 128 of the 256 rows of one index of ctx have a 0, and some index of ctx has exactly 128.
All inputs are finite; a program needn't handle non-finite values.
Results may differ from a plain program's by a relative error of at most 0.0097.
Values may be sent and summed in bfloat16 or wider, within the bound.
A program may use at most 128 MiB of HBM per device.

v0:
```python
import jax
import jax.numpy as jnp
from jax import lax
from jax.sharding import PartitionSpec as P

guidance_scale = 3.0


def sent_together(arrays, axis, dim, along):
    widths = [a.shape[along] for a in arrays]
    both = jnp.concatenate(arrays, axis=along)
    filled = lax.all_gather(both, axis, axis=dim, tiled=True)
    return tuple(jnp.split(filled, [sum(widths[:k]) for k in range(1, len(widths))], axis=along))


def norm_heads(values, gain):
    width = values.shape[-1]
    depth = gain.shape[0]
    lifted = values.astype(jnp.float32).reshape(values.shape[:-1] + (width // depth, depth))
    mean_square = jnp.mean(lifted * lifted, axis=-1, keepdims=True)
    scaled = lifted * lax.rsqrt(mean_square + 1e-06) * gain
    return scaled.reshape(values.shape).astype(jnp.bfloat16)


def absorb(state, keys_part, values_part, query_heads):
    heads = query_heads.shape[0]
    depth = query_heads.shape[2]
    length = keys_part.shape[0]
    block = 512
    key_blocks = keys_part.reshape(length // block, block, heads, depth)
    value_blocks = values_part.reshape(length // block, block, heads, depth)
    scale = depth ** (-0.5)

    def update(carried, blocks):
        summed, biggest, totals = carried
        keys_here, values_here = blocks
        scores = (
            jnp.einsum("hqd,khd->hqk", query_heads, keys_here, preferred_element_type=jnp.float32)
            * scale
        )
        newest = jnp.maximum(biggest, jnp.max(scores, axis=-1))
        factor = jnp.exp(biggest - newest)
        weights = jnp.exp(scores - newest[..., None])
        totals = totals * factor + jnp.sum(weights, axis=-1)
        added = jnp.einsum(
            "hqk,khd->hqd",
            weights.astype(jnp.bfloat16),
            values_here,
            preferred_element_type=jnp.float32,
        )
        summed = summed * factor[..., None] + added
        return ((summed, newest, totals), None)

    state, unused = lax.scan(update, state, (key_blocks, value_blocks))
    return state


def shards(
    query_proj,
    key_proj,
    value_proj,
    query_gain,
    key_gain,
    block_input,
    cached_out,
    replay_mask,
    branch_gate,
    attn_weight,
    final_shift,
    final_scale,
    patch_weight,
):
    count = query_proj.shape[1]
    width = query_proj.shape[2]
    depth = query_gain.shape[0]
    heads = width // depth
    live_count = count // 2
    share = count // lax.axis_size("tp")
    queries = norm_heads(query_proj[0], query_gain)
    keys_normed = norm_heads(key_proj[0], key_gain)
    values_local = value_proj[0]
    mask_local = replay_mask[0]
    selected = jnp.argsort(mask_local, stable=True)[:live_count]
    picked = queries[selected]
    picked_count = picked.shape[0]
    query_heads = picked.reshape(picked_count, heads, depth).transpose(1, 0, 2)
    start_state = (
        jnp.zeros((heads, picked_count, depth), jnp.float32),
        jnp.full((heads, picked_count), -1e30, jnp.float32),
        jnp.zeros((heads, picked_count), jnp.float32),
    )
    piece = sent_together((keys_normed, values_local), "ctx", 0, 1)
    state = absorb(start_state, piece[0], piece[1], query_heads)
    summed, biggest, totals = state
    attended_picked = (
        (summed / totals[..., None])
        .transpose(1, 0, 2)
        .reshape(picked_count, width)
        .astype(jnp.bfloat16)
    )
    attended = jnp.zeros((count, width), jnp.bfloat16).at[selected].set(attended_picked)
    projected = lax.psum_scatter(
        jnp.dot(attended, attn_weight, preferred_element_type=jnp.float32).astype(jnp.bfloat16),
        "tp",
        scatter_dimension=0,
        tiled=True,
    ).astype(jnp.float32)
    mask_rows = lax.dynamic_slice_in_dim(mask_local, lax.axis_index("tp") * share, share, 0)
    mixed = block_input[0].astype(jnp.float32) + branch_gate[0][None, :] * projected
    block_out = jnp.where(mask_rows[:, None] == 1, cached_out[0].astype(jnp.float32), mixed).astype(
        jnp.bfloat16
    )
    lifted = block_out.astype(jnp.float32)
    center = jnp.mean(lifted, axis=-1, keepdims=True)
    spread = jnp.mean((lifted - center) * (lifted - center), axis=-1, keepdims=True)
    normed = (
        (lifted - center) * lax.rsqrt(spread + 1e-06) * (1.0 + final_scale[0][None, :])
        + final_shift[0][None, :]
    ).astype(jnp.bfloat16)
    branch_out = jnp.dot(normed, patch_weight, preferred_element_type=jnp.float32)
    paired = lax.all_to_all(branch_out, "cfg", split_axis=1, concat_axis=0, tiled=True)
    cond_part = paired[:share]
    uncond_part = paired[share:]
    velocity = uncond_part + guidance_scale * (cond_part - uncond_part)
    return (block_out[None], velocity)


def solution(mesh):
    in_specs = (
        P("cfg", "ctx", "tp"),
        P("cfg", "ctx", "tp"),
        P("cfg", "ctx", "tp"),
        P(),
        P(),
        P("cfg", ("ctx", "tp"), None),
        P("cfg", ("ctx", "tp"), None),
        P("cfg", "ctx"),
        P("cfg", None),
        P("tp", None),
        P("cfg", None),
        P("cfg", None),
        P(),
    )
    out_specs = (P("cfg", ("ctx", "tp"), None), P(("ctx", "tp"), "cfg"))
    return jax.shard_map(shards, mesh=mesh, in_specs=in_specs, out_specs=out_specs, check_vma=False)
```

profile of v0, /device:TPU:16, one launch (start us, length us, event | category | flops | bytes accessed | tf_op | source)
XLA Modules:
  0.0 299.2 jit_solution(18116649159860371368)
XLA Ops:
  7.3 1.2 copy.30
  8.6 0.7 broadcast_bitcast_fusion.1
  9.2 1.1 copy.31
  10.4 0.8 pad_maximum_fusion
  11.3 1.0 convert_multiply_fusion
  12.3 0.2 copy.32
  12.5 0.8 mul.139
  13.3 1.2 copy.33
  14.5 3.2 %sort.17 = (s32[256]{0:T(256)}, s32[256]{0:T(256)S(1)}) sort(s32[256]{0:T(256)S(1)} %bitcast.110, s32[256]{0:T(256)S(1)} %iota.4), dimensions={0}, to_apply=%region_0.0 | sort | flops 2048 | bytes 4096 | tf_op jit(solution)/shard_map/jit(argsort)/sort | solution.py:83
  17.7 0.5 copy-done.9
  18.3 0.9 gather_fusion
  19.3 0.1 copy.36
  19.4 128.9 %all-gather.2.cloned.1.call-done = bf16[8192,768]{0,1:T(8,128)(2,1)} async-done(((bf16[256,768]{0,1:T(8,128)(2,1)}), bf16[8192,768]{0,1:T(8,128)(2,1)}) %all-gather.2.cloned.1.call-update) | async-done | bytes 12582928 | tf_op jit(solution)/shard_map/all_gather | solution.py:12
  148.3 8.2 %fusion.39 = (bf16[8192,384]{0,1:T(8,128)(2,1)}, bf16[8192,384]{0,1:T(8,128)(2,1)S(1)}) fusion(bf16[8192,768]{0,1:T(8,128)(2,1)} %all-gather.2.cloned.1.call-done), kind=kLoop, calls=%fused_computation.67 | loop fusion | bytes 25165824 | tf_op jit(solution)/shard_map/split | solution.py:13
  156.6 5.6 %copy.42 = bf16[48,8,16,512]{3,2,1,0:T(8,128)(2,1)} copy(bf16[48,8,16,512]{3,1,2,0:T(8,128)(2,1)S(1)} %bitcast.99) | data formatting | bytes 12582912
  162.1 9.1 %copy.35 = bf16[16,512,3,128]{3,1,2,0:T(8,128)(2,1)} copy(bf16[16,512,3,128]{1,0,3,2:T(8,128)(2,1)} %bitcast.96) | data formatting | bytes 12582912
  171.3 8.3 %copy.43 = bf16[48,8,16,512]{3,2,1,0:T(8,128)(2,1)} copy(bf16[48,8,16,512]{3,1,2,0:T(8,128)(2,1)} %bitcast.98) | data formatting | bytes 12582912
  179.6 9.2 %copy.37 = bf16[16,512,3,128]{3,1,2,0:T(8,128)(2,1)} copy(bf16[16,512,3,128]{1,0,3,2:T(8,128)(2,1)} %bitcast.97) | data formatting | bytes 12582912
  188.7 45.7 %while.15 = (s32[]{:T(128)}, f32[3,128,128]{2,1,0:T(8,128)S(1)}, f32[3,128]{1,0:T(4,128)S(1)}, f32[3,128]{1,0:T(4,128)S(1)}, bf16[16,512,3,128]{3,1,2,0:T(8,128)...) while((s32[]{:T(128)}, f32[3,128,128]{2,1,0:T(8,128)S(1)}, ...), condition=%wide.region_6.7_spmd.clone, body=%wide.region_3.6_spmd.clone.sunk | while | flops 101992320 | bytes 3662953 | solution.py:54
  188.7 1.3 fusion.53
  190.2 1.4 convolution_add_fusion.2
  191.6 1.3 fusion.53
  193.0 1.4 convolution_add_fusion.2
  194.4 1.3 fusion.53
  195.9 1.4 convolution_add_fusion.2
  197.3 1.3 fusion.53
  198.7 1.4 convolution_add_fusion.2
  200.1 1.3 fusion.53
  201.6 1.4 convolution_add_fusion.2
  203.0 1.3 fusion.53
  204.4 1.4 convolution_add_fusion.2
  205.8 1.3 fusion.53
  207.1 0.1 fusion.54
  207.3 1.4 convolution_add_fusion.2
  208.7 1.3 fusion.53
  210.1 1.4 convolution_add_fusion.2
  211.5 1.3 fusion.53
  213.0 1.4 convolution_add_fusion.2
  214.4 1.3 fusion.53
  215.9 1.4 convolution_add_fusion.2
  217.3 1.3 fusion.53
  218.7 1.4 convolution_add_fusion.2
  220.1 1.3 fusion.53
  221.6 1.4 convolution_add_fusion.2
  223.0 1.3 fusion.53
  224.3 0.1 fusion.54
  224.4 1.4 convolution_add_fusion.2
  225.8 1.3 fusion.53
  227.3 1.4 convolution_add_fusion.2
  228.7 1.3 fusion.53
  230.1 1.4 convolution_add_fusion.2
  231.5 1.3 fusion.53
  233.0 1.4 convolution_add_fusion.2
  234.4 0.1 copy.38
  234.7 1.2 scatter_custom_fusion
  236.0 2.1 convolution_convert_fusion
  238.2 43.0 %reduce-scatter.2.cloned.1.call-done = bf16[32,3072]{1,0:T(8,128)(2,1)} async-done(((bf16[256,3072]{1,0:T(8,128)(2,1)}), bf16[32,3072]{1,0:T(8,128)(2,1)}) %reduce-scatter.2.cloned.1.call-update) | async-done | bytes 196624 | tf_op jit(solution)/shard_map/reduce_scatter | solution.py:102
  281.2 1.1 convert_reduce_fusion
  282.4 0.2 fusion.14
  282.6 1.3 fusion.26
  284.1 6.3 %all_to_all.16 = f32[2,1,1024]{2,1,0:T(1,128)S(1)} all-to-all(f32[2,1,1024]{2,1,0:T(1,128)S(1)} %reshape.115), channel_id=1, replica_groups=mesh['cfg'=2,'ctx'=32,'tp'=8] {'cfg'}, dimensions={0} | all-to-all | bytes 16384 | tf_op jit(solution)/shard_map/all_to_all | solution.py:121
  290.5 0.5 broadcast.118
  291.0 0.7 reduce
  291.8 0.6 fusion.36
  (113 shorter events, 3.3 us)
Async XLA Ops:
  7.2 228.8 %copy-start = (bf16[384,3072]{1,0:T(8,128)(2,1)S(1)}, bf16[384,3072]{1,0:T(8,128)(2,1)}, u32[]{:S(2)}) copy-start(bf16[384,3072]{1,0:T(8,128)(2,1)} %param.24) | copy-start | bytes 7077892
  7.2 11.0 %copy-start.2 = (bf16[1,256,384]{2,1,0:T(8,128)(2,1)S(1)}, bf16[1,256,384]{2,1,0:T(8,128)(2,1)}, u32[]{:S(2)}) copy-start(bf16[1,256,384]{2,1,0:T(8,128)(2,1)} %param.15) | copy-start | bytes 589828
  7.2 7.3 %copy-start.7 = (s32[1,256]{1,0:T(1,128)S(1)}, s32[1,256]{1,0:T(1,128)}, u32[]{:S(2)}) copy-start(s32[1,256]{1,0:T(1,128)} %param.22) | copy-start | bytes 3076
  7.2 11.0 %copy-start.8 = (f32[128]{0:T(128)S(1)}, f32[128]{0:T(128)}, u32[]{:S(2)}) copy-start(f32[128]{0:T(128)} %param.18) | copy-start | bytes 1540
  7.2 141.1 %all-gather.2.cloned.1.call-start = ((), (), s32[]{:S(2)}) async-start(), calls=%async_computation.2 | async-start | bytes 12976128 | tf_op jit(solution)/shard_map/all_gather | solution.py:12
  11.2 270.0 %reduce-scatter.2.cloned.1.call-start = ((), (), s32[]{:S(2)}) async-start(), calls=%async_computation.3 | async-start | bytes 1769472 | tf_op jit(solution)/shard_map/reduce_scatter | solution.py:102
  17.7 0.5 copy-start.9
  234.4 3.8 %copy-start.5 = (f32[1,3072]{1,0:T(1,128)S(1)}, f32[1,3072]{1,0:T(1,128)}, u32[]{:S(2)}) copy-start(f32[1,3072]{1,0:T(1,128)} %param.26) | copy-start | bytes 36868
  234.4 46.8 %copy-start.3 = (bf16[1,32,3072]{2,1,0:T(8,128)(2,1)S(1)}, bf16[1,32,3072]{2,1,0:T(8,128)(2,1)}, u32[]{:S(2)}) copy-start(bf16[1,32,3072]{2,1,0:T(8,128)(2,1)} %param.20) | copy-start | bytes 589828
  234.4 46.8 %copy-start.4 = (bf16[1,32,3072]{2,1,0:T(8,128)(2,1)S(1)}, bf16[1,32,3072]{2,1,0:T(8,128)(2,1)}, u32[]{:S(2)}) copy-start(bf16[1,32,3072]{2,1,0:T(8,128)(2,1)} %param.21) | copy-start | bytes 589828
  234.4 46.8 %copy-start.6 = (f32[1,3072]{1,0:T(1,128)S(1)}, f32[1,3072]{1,0:T(1,128)}, u32[]{:S(2)}) copy-start(f32[1,3072]{1,0:T(1,128)} %param.23) | copy-start | bytes 36868
  234.4 48.2 %copy-start.10 = (f32[1,3072]{1,0:T(1,128)S(1)}, f32[1,3072]{1,0:T(1,128)}, u32[]{:S(2)}) copy-start(f32[1,3072]{1,0:T(1,128)} %param.25) | copy-start | bytes 36868
  282.4 10.0 %copy-start.1 = (bf16[32,3072]{1,0:T(8,128)(2,1)}, bf16[32,3072]{1,0:T(8,128)(2,1)S(1)}, u32[]{:S(2)}) copy-start(bf16[32,3072]{1,0:T(8,128)(2,1)S(1)} %get-tuple-element.99) | copy-start | bytes 589828
Sparse Core Ops, SparseCore 0:
  11.4 136.9 all-gather.1
  238.3 42.9 reduce-scatter.1
where the time goes:
time: 301 us; the launch traced here: 299 us
  waiting for transfers between devices  172 us (57%)
  local copies, waits for them, and re-layouts  49.4 us (16%)
  matrix products  45.9 us (15%)
  between operations  14.3 us (5%)
  other arithmetic  10.4 us (3%)
  blocking collectives  6.35 us (2%)
    all_gather x1, waiting for transfers between devices, sent_together(): filled = lax.all_gather(both, axis, axis=dim, tiled=True)  129 us
    reduce_scatter x1, waiting for transfers between devices, shards(): lax.psum_scatter(jnp.dot(attended, attn_weight, preferred_element_type=jn...  43 us
    unnamed x31, local copies, waits for them, and re-layouts  35.3 us
    dot_general x16, matrix products, update(): jnp.einsum('hqk,khd->hqd', weights.astype(jnp.bfloat16), values_here, pre...  22 us
    dot_general x16, matrix products, update(): jnp.einsum('hqd,khd->hqk', query_heads, keys_here, preferred_element_type...  20.5 us
    split x1, local copies, waits for them, and re-layouts, sent_together(): jnp.split(filled, [sum(widths[:k]) for k in range(1, len(widths))], axis=...  8.21 us
    all_to_all x1, blocking collectives, shards(): lax.all_to_all(branch_out, 'cfg', split_axis=1, concat_axis=0, tiled=True)  6.35 us
  transfers between devices with their start and end apart: 2, of which 2 were waited for; matrix products, arithmetic and copies ran while one was open for 3% of the time, Pallas kernels for 0%

commit v1 on v0

v1 whole, which is shorter than its diff:
```python
import functools
import math

import jax
import jax.numpy as jnp
from jax import lax
from jax.experimental import pallas as pl
from jax.experimental.pallas import tpu as pltpu
from jax.sharding import PartitionSpec as P

guidance_scale = 3.0
f32 = jnp.float32
bf16 = jnp.bfloat16
cut = 512


def dot(a, b, contract=(1, 0)):
    return lax.dot_general(
        a, b, (((contract[0],), (contract[1],)), ((), ())), preferred_element_type=f32
    )


def remote(src, dst, sems, index, device):
    return pltpu.make_async_remote_copy(
        src_ref=src,
        dst_ref=dst,
        send_sem=sems[0].at[index],
        recv_sem=sems[1].at[index],
        device_id=device,
        device_id_type=pl.DeviceIdType.MESH,
    )


def kernel(
    ny,
    nz,
    q_ref,
    k_ref,
    v_ref,
    qg_ref,
    kg_ref,
    mask_ref,
    gate_ref,
    shift_ref,
    scale_ref,
    bi_hbm,
    co_hbm,
    w_hbm,
    pw_hbm,
    bo_hbm,
    vel_ref,
    bi_ref,
    co_ref,
    w_ref,
    pw_ref,
    bo_ref,
    sel_ref,
    kbuf,
    vbuf,
    rk,
    rv,
    qbuf,
    oacc,
    stat,
    own_o,
    own_s,
    osnd,
    orcv,
    att_ref,
    pbuf,
    zsnd,
    zrcv,
    ysnd,
    yrcv,
    loc_sem,
    qs,
    qr,
    ks,
    kr,
    os_,
    or_,
    zs,
    zr,
    ys,
    yr,
):
    count, width = q_ref.shape
    depth = qg_ref.shape[1]
    heads = width // depth
    live = qbuf.shape[3]
    share, feats = bi_ref.shape
    cuts = feats // cut
    c2 = depth ** (-0.5) * math.log2(math.e)
    yh, zh = ny // 2, nz // 2

    cfg = lax.axis_index("cfg")
    ctx = lax.axis_index("ctx")
    tp = lax.axis_index("tp")
    core = lax.rem(ctx, 2)
    hi = lax.rem(lax.div(ctx, 2), 2)
    y = lax.div(ctx, 4)
    x = hi * 2 + cfg

    def at_x(place):
        return {"cfg": lax.rem(place, 2), "ctx": y * 4 + lax.div(place, 2) * 2 + core}

    x_up, x_dn = at_x(lax.rem(x + 1, 4)), at_x(lax.rem(x + 3, 4))
    sib = {"ctx": ctx + 1 - 2 * core}
    y_up = {"ctx": lax.rem(y + 1, ny) * 4 + hi * 2 + core}
    y_dn = {"ctx": lax.rem(y + ny - 1, ny) * 4 + hi * 2 + core}
    z_up = {"tp": lax.rem(tp + 1, nz)}
    z_dn = {"tp": lax.rem(tp + nz - 1, nz)}
    other = {"cfg": 1 - cfg}

    barrier = pltpu.get_barrier_semaphore()
    for device in (x_up, x_dn, sib, y_up, y_dn, z_up, z_dn):
        pl.semaphore_signal(
            barrier, inc=1, device_id=device, device_id_type=pl.DeviceIdType.MESH
        )

    loads = [
        pltpu.make_async_copy(src, dst, loc_sem.at[n])
        for n, (src, dst) in enumerate(
            ((w_hbm, w_ref), (bi_hbm, bi_ref), (co_hbm, co_ref), (pw_hbm, pw_ref))
        )
    ]
    for load in loads:
        load.start()

    def q_up(s, h):
        return remote(
            qbuf.at[lax.rem(ny - s, ny), h], qbuf.at[ny - 1 - s, h], (qs, qr), (0, s, h), y_up
        )

    def q_dn(s, h):
        return remote(qbuf.at[s, h], qbuf.at[s + 1, h], (qs, qr), (1, s, h), y_dn)

    kv = (ks, kr)

    def k_sib(h):
        return remote(kbuf.at[0, h], kbuf.at[1, h], kv, (0, h), sib)

    def v_sib(h):
        return remote(vbuf.at[0, h], vbuf.at[1, h], kv, (1, h), sib)

    def k_out(h):
        return remote(kbuf.at[0, h], rk.at[h], kv, (2, h), x_up)

    def v_out(h):
        return remote(vbuf.at[0, h], rv.at[h], kv, (3, h), x_dn)

    def k_on(h):
        return remote(rk.at[h], kbuf.at[2, h], kv, (4, h), x_up)

    def v_on(h):
        return remote(rv.at[h], vbuf.at[2, h], kv, (5, h), x_dn)

    def k_last(h):
        return remote(kbuf.at[2, h], kbuf.at[3, h], kv, (6, h), sib)

    def v_last(h):
        return remote(vbuf.at[2, h], vbuf.at[3, h], kv, (7, h), sib)

    def o_up(s, h):
        return remote(osnd.at[0, s, h], orcv.at[0, s, h], (os_, or_), (0, s, h), y_up)

    def o_dn(s, h):
        return remote(osnd.at[1, s, h], orcv.at[1, s, h], (os_, or_), (1, s, h), y_dn)

    def z_upc(s, n):
        return remote(zsnd.at[0, s, n], zrcv.at[0, s, n], (zs, zr), (0, s, n), z_up)

    def z_dnc(s, n):
        return remote(zsnd.at[1, s, n], zrcv.at[1, s, n], (zs, zr), (1, s, n), z_dn)

    alive = (mask_ref[...] == 0).astype(f32)
    alive8 = jnp.broadcast_to(alive, (8, count))
    before = (
        lax.broadcasted_iota(jnp.int32, (count, count), 0)
        < lax.broadcasted_iota(jnp.int32, (count, count), 1)
    ).astype(f32)
    rank = dot(alive8.astype(bf16), before.astype(bf16))[0:1]
    slot = lax.broadcasted_iota(jnp.int32, (live, count), 0).astype(f32)
    picks = jnp.where((slot == rank) & (alive > 0.5), 1.0, 0.0)
    sel_ref[...] = picks.T.astype(bf16)
    picks = picks.astype(bf16)

    def normed_head(ref, gain_ref, h):
        part = ref[:, h * depth : (h + 1) * depth].astype(f32)
        square = jnp.mean(part * part, axis=-1, keepdims=True)
        return part * lax.rsqrt(square + 1e-06) * gain_ref[...]

    for h in range(heads):
        qn = normed_head(q_ref, qg_ref, h).astype(bf16)
        qbuf[0, h] = dot(picks, qn).T.astype(bf16)
        kbuf[0, h] = normed_head(k_ref, kg_ref, h).astype(bf16)
        vbuf[0, h] = v_ref[:, h * depth : (h + 1) * depth].astype(f32).T.astype(bf16)
        if h == 0:
            pl.semaphore_wait(barrier, 7)
        k_out(h).start()
        v_out(h).start()
        q_up(0, h).start()
        q_dn(0, h).start()
        k_sib(h).start()
        v_sib(h).start()

    def half(h, a, b, first):
        pair = (0, 1) if first else (2, 3)
        q2 = jnp.concatenate([qbuf[a, h], qbuf[b, h]], axis=1)
        scores = [dot(kbuf[j, h], q2) for j in pair]
        top = jnp.maximum(*[jnp.max(s, axis=0, keepdims=True) for s in scores])
        top = top.astype(bf16).astype(f32)
        if not first:
            old = jnp.concatenate([stat[a, h, 0:1], stat[b, h, 0:1]], axis=1)
            top = jnp.maximum(top, old)
        weights = [jnp.exp2((s - top) * c2) for s in scores]
        total = sum(jnp.sum(w, axis=0, keepdims=True) for w in weights)
        summed = sum(dot(vbuf[j, h], w.astype(bf16)) for j, w in zip(pair, weights))
        if not first:
            factor = jnp.exp2((old - top) * c2)
            total += factor * jnp.concatenate([stat[a, h, 1:2], stat[b, h, 1:2]], axis=1)
            summed += factor * jnp.concatenate([oacc[a, h], oacc[b, h]], axis=1)
        return summed, top, total

    def q_step(s, carry):
        a, b = ny - 1 - s, lax.rem(s + 1, yh)
        for h in range(heads):
            q_up(s, h).wait_recv()

            @pl.when(s < yh - 1)
            def _():
                q_up(s + 1, h).start()
                q_dn(s, h).wait_recv()

            @pl.when(s < yh - 2)
            def _():
                q_dn(s + 1, h).start()

            @pl.when(s == 0)
            def _():
                k_out(h).wait_recv()
                k_on(h).start()
                v_out(h).wait_recv()
                v_on(h).start()
                k_sib(h).wait_recv()
                v_sib(h).wait_recv()

            @pl.when(s == 1)
            def _():
                k_on(h).wait_recv()
                k_last(h).start()
                v_on(h).wait_recv()
                v_last(h).start()

            summed, top, total = half(h, a, b, True)
            for n, place in enumerate((a, b)):
                lanes = slice(n * live, (n + 1) * live)
                oacc[place, h] = summed[:, lanes]
                stat[place, h, 0:1] = top[:, lanes]
                stat[place, h, 1:2] = total[:, lanes]
        return carry

    lax.fori_loop(0, yh, q_step, 0)

    for h in range(heads):
        k_last(h).wait_recv()
        v_last(h).wait_recv()

    def put(way, s, h, summed, top, total):
        osnd[way, s, h, 0:depth] = summed.astype(bf16)
        high = total.astype(bf16).astype(f32)
        row = lax.broadcasted_iota(jnp.int32, (16, live), 0)
        tile = jnp.where(row == 0, top, jnp.where(row == 1, high, total - high))
        osnd[way, s, h, depth : depth + 16] = tile.astype(bf16)

    def merge(way, s, h, summed, top, total):
        theirs = orcv[way, s, h, 0:depth].astype(f32)
        tile = orcv[way, s, h, depth : depth + 16].astype(f32)
        their_top, their_total = tile[0:1], tile[1:2] + tile[2:3]
        newest = jnp.maximum(top, their_top)
        mine, factor = jnp.exp2((top - newest) * c2), jnp.exp2((their_top - newest) * c2)
        return summed * mine + theirs * factor, newest, total * mine + their_total * factor

    def split(parts, n):
        return [part[:, n * live : (n + 1) * live] for part in parts]

    for h in range(heads):
        parts = half(h, yh, yh + 1, False)
        put(0, 0, h, *split(parts, 0))
        o_up(0, h).start()
        put(1, 0, h, *split(parts, 1))
        o_dn(0, h).start()

    def o_step(s, carry):
        for h in range(heads):
            parts = half(h, yh - s, lax.rem(yh + 1 + s, ny), False)
            o_up(s - 1, h).wait_recv()
            put(0, s, h, *merge(0, s - 1, h, *split(parts, 0)))
            o_up(s, h).start()
            o_dn(s - 1, h).wait_recv()
            summed, top, total = merge(1, s - 1, h, *split(parts, 1))

            @pl.when(s < yh - 1)
            def _():
                put(1, s, h, summed, top, total)
                o_dn(s, h).start()

            own_o[h] = summed
            own_s[h, 0:1] = top
            own_s[h, 1:2] = total
        return carry

    lax.fori_loop(1, yh, o_step, 0)

    for h in range(heads):
        o_up(yh - 1, h).wait_recv()
        summed, top, total = merge(0, yh - 1, h, own_o[h], own_s[h, 0:1], own_s[h, 1:2])
        done = (summed / total).astype(bf16)
        att_ref[:, h * depth : (h + 1) * depth] = dot(sel_ref[...], done, (1, 1)).astype(bf16)

    loads[0].wait()

    def rows_of(n, place):
        start = pl.multiple_of(place * share, share)
        return pbuf[n, pl.ds(start, share), :]

    def z_first(n, carry):
        columns = pl.ds(pl.multiple_of(n * cut, cut), cut)
        pbuf[n] = dot(att_ref[...], w_ref[:, columns])
        zsnd[0, 0, n] = rows_of(n, lax.rem(tp + zh, nz)).astype(bf16)
        z_upc(0, n).start()
        zsnd[1, 0, n] = rows_of(n, lax.rem(tp + zh + 1, nz)).astype(bf16)
        z_dnc(0, n).start()
        return carry

    lax.fori_loop(0, cuts, z_first, 0)

    def z_step(s, carry):
        def z_cut(n, inner):
            z_upc(s - 1, n).wait_recv()
            part = rows_of(n, lax.rem(tp + zh - s, nz))
            zsnd[0, s, n] = (part + zrcv[0, s - 1, n].astype(f32)).astype(bf16)
            z_upc(s, n).start()

            @pl.when(s < zh - 1)
            def _():
                z_dnc(s - 1, n).wait_recv()
                part = rows_of(n, lax.rem(tp + zh + 1 + s, nz))
                zsnd[1, s, n] = (part + zrcv[1, s - 1, n].astype(f32)).astype(bf16)
                z_dnc(s, n).start()

            return inner

        return lax.fori_loop(0, cuts, z_cut, carry)

    lax.fori_loop(1, zh, z_step, 0)

    loads[1].wait()
    loads[2].wait()
    loads[3].wait()
    own_rows = pl.ds(pl.multiple_of(tp * share, share), share)
    alive_rows = jnp.sum(sel_ref[own_rows, :].astype(f32), axis=1, keepdims=True) > 0.5
    sums = jnp.zeros((share, 1), f32)
    for n in range(cuts):
        columns = slice(n * cut, (n + 1) * cut)
        z_upc(zh - 1, n).wait_recv()
        z_dnc(zh - 2, n).wait_recv()
        projected = (
            rows_of(n, tp) + zrcv[0, zh - 1, n].astype(f32) + zrcv[1, zh - 2, n].astype(f32)
        )
        mixed = bi_ref[:, columns].astype(f32) + gate_ref[:, columns] * projected
        out = jnp.where(alive_rows, mixed, co_ref[:, columns].astype(f32)).astype(bf16)
        bo_ref[:, columns] = out
        sums += jnp.sum(out.astype(f32), axis=1, keepdims=True)
    store = pltpu.make_async_copy(bo_ref, bo_hbm, loc_sem.at[4])
    store.start()
    center = sums * (1.0 / feats)
    away = bo_ref[...].astype(f32) - center
    spread = jnp.mean(away * away, axis=1, keepdims=True)
    normed = away * lax.rsqrt(spread + 1e-06) * (1.0 + scale_ref[...]) + shift_ref[...]
    ysnd[...] = dot(normed.astype(bf16), pw_ref[...], (1, 1))
    swap = remote(ysnd, yrcv, (ys, yr), 0, other)
    swap.start()
    swap.wait_recv()
    mine, theirs = ysnd[...], yrcv[...]
    cond = jnp.where(cfg == 0, mine, theirs)
    uncond = jnp.where(cfg == 0, theirs, mine)
    velocity = uncond + guidance_scale * (cond - uncond)
    half_width = vel_ref.shape[1]
    vel_ref[...] = jnp.where(cfg == 0, velocity[:, :half_width], velocity[:, half_width:])

    store.wait()
    swap.wait_send()
    for h in range(heads):
        for copy in (k_sib, v_sib, k_out, v_out, k_on, v_on, k_last, v_last):
            copy(h).wait_send()

    def drain(s, carry):
        for h in range(heads):
            q_up(s, h).wait_send()
            o_up(s, h).wait_send()

            @pl.when(s < yh - 1)
            def _():
                q_dn(s, h).wait_send()
                o_dn(s, h).wait_send()

        return carry

    lax.fori_loop(0, yh, drain, 0)

    def z_drain(s, carry):
        def one(n, inner):
            z_upc(s, n).wait_send()

            @pl.when(s < zh - 1)
            def _():
                z_dnc(s, n).wait_send()

            return inner

        return lax.fori_loop(0, cuts, one, carry)

    lax.fori_loop(0, zh, z_drain, 0)


def shards(
    query_proj,
    key_proj,
    value_proj,
    query_gain,
    key_gain,
    block_input,
    cached_out,
    replay_mask,
    branch_gate,
    attn_weight,
    final_shift,
    final_scale,
    patch_weight,
):
    ny = lax.axis_size("ctx") // 4
    nz = lax.axis_size("tp")
    count, width = query_proj.shape[1:]
    depth = query_gain.shape[0]
    heads = width // depth
    live = count // 2
    share, feats = block_input.shape[1:]
    channels = patch_weight.shape[1]
    yh, zh = ny // 2, nz // 2
    cuts = feats // cut
    vmem = pl.BlockSpec(memory_space=pltpu.VMEM)
    anywhere = pl.BlockSpec(memory_space=pl.ANY)
    dma = pltpu.SemaphoreType.DMA
    block_out, velocity = pl.pallas_call(
        functools.partial(kernel, ny, nz),
        out_shape=(
            jax.ShapeDtypeStruct((share, feats), bf16),
            jax.ShapeDtypeStruct((share, channels // 2), f32),
        ),
        in_specs=[vmem] * 9 + [anywhere] * 4,
        out_specs=(anywhere, vmem),
        scratch_shapes=[
            pltpu.VMEM((share, feats), bf16),
            pltpu.VMEM((share, feats), bf16),
            pltpu.VMEM((width, feats), bf16),
            pltpu.VMEM((channels, feats), bf16),
            pltpu.VMEM((share, feats), bf16),
            pltpu.VMEM((count, live), bf16),
            pltpu.VMEM((4, heads, count, depth), bf16),
            pltpu.VMEM((4, heads, depth, count), bf16),
            pltpu.VMEM((heads, count, depth), bf16),
            pltpu.VMEM((heads, depth, count), bf16),
            pltpu.VMEM((ny, heads, depth, live), bf16),
            pltpu.VMEM((ny, heads, depth, live), f32),
            pltpu.VMEM((ny, heads, 8, live), f32),
            pltpu.VMEM((heads, depth, live), f32),
            pltpu.VMEM((heads, 8, live), f32),
            pltpu.VMEM((2, yh, heads, depth + 16, live), bf16),
            pltpu.VMEM((2, yh, heads, depth + 16, live), bf16),
            pltpu.VMEM((count, width), bf16),
            pltpu.VMEM((cuts, count, cut), f32),
            pltpu.VMEM((2, zh, cuts, share, cut), bf16),
            pltpu.VMEM((2, zh, cuts, share, cut), bf16),
            pltpu.VMEM((share, channels), f32),
            pltpu.VMEM((share, channels), f32),
            dma((5,)),
            dma((2, yh, heads)),
            dma((2, yh, heads)),
            dma((8, heads)),
            dma((8, heads)),
            dma((2, yh, heads)),
            dma((2, yh, heads)),
            dma((2, zh, cuts)),
            dma((2, zh, cuts)),
            dma((1,)),
            dma((1,)),
        ],
        compiler_params=pltpu.CompilerParams(
            collective_id=0, has_side_effects=True, vmem_limit_bytes=56 * 1024 * 1024
        ),
        name="block",
    )(
        query_proj[0],
        key_proj[0],
        value_proj[0],
        query_gain[None],
        key_gain[None],
        replay_mask,
        branch_gate,
        final_shift,
        final_scale,
        block_input[0],
        cached_out[0],
        attn_weight,
        patch_weight.T,
    )
    return (block_out[None], velocity)


def solution(mesh):
    in_specs = (
        P("cfg", "ctx", "tp"),
        P("cfg", "ctx", "tp"),
        P("cfg", "ctx", "tp"),
        P(),
        P(),
        P("cfg", ("ctx", "tp"), None),
        P("cfg", ("ctx", "tp"), None),
        P("cfg", "ctx"),
        P("cfg", None),
        P("tp", None),
        P("cfg", None),
        P("cfg", None),
        P(),
    )
    out_specs = (P("cfg", ("ctx", "tp"), None), P(("ctx", "tp"), "cfg"))
    return jax.shard_map(shards, mesh=mesh, in_specs=in_specs, out_specs=out_specs, check_vma=False)
```

time: 301 us -> 74.2 us (0.25)
  the two profiles are of different devices: /device:TPU:16 before, /device:TPU:2 now
where the time goes in v1:
time: 74.2 us; the launch traced here: 74 us
  Pallas kernels  70.4 us (95%)
  local copies, waits for them, and re-layouts  2.94 us (4%)
    pallas_call x1, Pallas kernels, shards(): pl.pallas_call(functools.partial(kernel, ny, nz), out_shape=(jax.ShapeDty...  70.4 us
    unnamed x2, local copies, waits for them, and re-layouts  2.94 us

profile of v1, /device:TPU:2, one launch (start us, length us, event | category | flops | bytes accessed | tf_op | source)
XLA Modules:
  0.0 74.0 jit_solution(15002554363606366486)
XLA Ops:
  0.6 70.4 %block.1 = (bf16[32,3072]{1,0:T(8,128)(2,1)}, f32[32,32]{1,0:T(8,128)}) custom-call(bf16[256,384]{1,0:T(8,128)(2,1)} %bitcast.10, bf16[256,384]{1,0:T(8,128)(2,1)} %bitcast.11, bf16[256,384]{1,0:T(8,128)(2,1)} %bitcast.12, f32[1,128]{1,0:T(1,128)} %bitcast.16, f32[1,128]{1,0:T(1,128)} %bitcast.17, s32[1,256]{1,0:T(1,128)} %mask_ref.1, f32[1,3072]{1,0:T(1,128)} %gate_ref.1, ...), custom_call_target="tpu_custom_call" | custom-call | tf_op jit(solution)/shard_map/block/pallas_call | solution.py:455
  71.0 1.6 %copy.17 = bf16[1,32,3072]{2,1,0:T(8,128)(2,1)} copy(bf16[1,32,3072]{2,1,0:T(8,128)(2,1)} %bitcast.15) | data formatting | bytes 393216
  72.6 1.3 %copy.18 = f32[32,32]{1,0:T(8,128)} copy(f32[32,32]{1,0:T(8,128)} %get-tuple-element.9) | data formatting | bytes 8192

commit v2 on v1

v2 whole, which is shorter than its diff:
```python
import functools
import math

import jax
import jax.numpy as jnp
from jax import lax
from jax.experimental import pallas as pl
from jax.experimental.pallas import tpu as pltpu
from jax.sharding import PartitionSpec as P

guidance_scale = 3.0
f32 = jnp.float32
bf16 = jnp.bfloat16
cut = 512


def dot(a, b, contract=(1, 0)):
    return lax.dot_general(
        a, b, (((contract[0],), (contract[1],)), ((), ())), preferred_element_type=f32
    )


def remote(src, dst, sems, kind, index, device):
    return pltpu.make_async_remote_copy(
        src_ref=src,
        dst_ref=dst,
        send_sem=sems[0].at[kind],
        recv_sem=sems[1].at[index],
        device_id=device,
        device_id_type=pl.DeviceIdType.MESH,
    )


def kernel(
    ny,
    nz,
    q_hbm,
    k_hbm,
    v_hbm,
    qg_hbm,
    kg_hbm,
    mask_hbm,
    gate_hbm,
    shift_hbm,
    scale_hbm,
    bi_hbm,
    co_hbm,
    w_hbm,
    pw_hbm,
    bo_out,
    vel_out,
    bo_ref,
    vel_ref,
    q_ref,
    k_ref,
    v_ref,
    qg_ref,
    kg_ref,
    mask_ref,
    gate_ref,
    shift_ref,
    scale_ref,
    bi_ref,
    co_ref,
    w_ref,
    pw_ref,
    sel_ref,
    kbuf,
    vbuf,
    rk,
    rv,
    qbuf,
    oacc,
    stat,
    part_o,
    part_s,
    own_o,
    own_s,
    osnd,
    orcv,
    att_ref,
    pbuf,
    zsnd,
    zrcv,
    ysnd,
    yrcv,
    loc_sem,
    left,
    qr,
    kr,
    or_,
    zr,
    yr,
):
    count, width = q_ref.shape
    depth = qg_ref.shape[1]
    heads = width // depth
    live = qbuf.shape[3]
    share, feats = bi_ref.shape
    cuts = feats // cut
    c2 = depth ** (-0.5) * math.log2(math.e)
    yh, zh = ny // 2, nz // 2

    cfg = lax.axis_index("cfg")
    ctx = lax.axis_index("ctx")
    tp = lax.axis_index("tp")
    core = lax.rem(ctx, 2)
    hi = lax.rem(lax.div(ctx, 2), 2)
    y = lax.div(ctx, 4)
    x = hi * 2 + cfg

    def at_x(place):
        return {"cfg": lax.rem(place, 2), "ctx": y * 4 + lax.div(place, 2) * 2 + 1 - core}

    x_up, x_dn = at_x(lax.rem(x + 1, 4)), at_x(lax.rem(x + 3, 4))
    sib = {"ctx": ctx + 1 - 2 * core}
    y_up = {"ctx": lax.rem(y + 1, ny) * 4 + hi * 2 + 1 - core}
    y_dn = {"ctx": lax.rem(y + ny - 1, ny) * 4 + hi * 2 + 1 - core}
    z_up = {"tp": lax.rem(tp + 1, nz)}
    z_dn = {"tp": lax.rem(tp + nz - 1, nz)}
    other = {"cfg": 1 - cfg}

    barrier = pltpu.get_barrier_semaphore()
    for device in (x_up, x_dn, sib, y_up, y_dn, z_up, z_dn, other):
        pl.semaphore_signal(
            barrier, inc=1, device_id=device, device_id_type=pl.DeviceIdType.MESH
        )

    pairs = (
        (mask_hbm, mask_ref),
        (q_hbm, q_ref),
        (qg_hbm, qg_ref),
        (k_hbm, k_ref),
        (kg_hbm, kg_ref),
        (v_hbm, v_ref),
        (w_hbm, w_ref),
        (bi_hbm, bi_ref),
        (co_hbm, co_ref),
        (gate_hbm, gate_ref),
        (scale_hbm, scale_ref),
        (shift_hbm, shift_ref),
        (pw_hbm, pw_ref),
    )
    loads = [
        pltpu.make_async_copy(src, dst, loc_sem.at[n]) for n, (src, dst) in enumerate(pairs)
    ]
    for load in loads:
        load.start()

    def q_up(s, h):
        return remote(
            qbuf.at[lax.rem(ny - s, ny), h], qbuf.at[ny - 1 - s, h], (left, qr), 0, (s, h), y_up
        )

    def q_dn(s, h):
        return remote(qbuf.at[s, h], qbuf.at[s + 1, h], (left, qr), 0, (yh + s, h), y_dn)

    kv = (left, kr)
    first_leg, second_leg = heads, 2 * heads

    def k_sib(h):
        return remote(kbuf.at[0, h], kbuf.at[1, h], kv, 1, 0, sib)

    def v_sib(h):
        return remote(vbuf.at[0, h], vbuf.at[1, h], kv, 2, 0, sib)

    def k_out(h):
        return remote(kbuf.at[0, h], rk.at[h], kv, 1, first_leg + h, x_up)

    def v_out(h):
        return remote(vbuf.at[0, h], rv.at[h], kv, 2, first_leg + h, x_dn)

    def k_on(h):
        return remote(rk.at[h], kbuf.at[2, h], kv, 1, second_leg + h, x_up)

    def v_on(h):
        return remote(rv.at[h], vbuf.at[2, h], kv, 2, second_leg + h, x_dn)

    def k_last(h):
        return remote(kbuf.at[2, h], kbuf.at[3, h], kv, 1, 1, sib)

    def v_last(h):
        return remote(vbuf.at[2, h], vbuf.at[3, h], kv, 2, 1, sib)

    def kv_come(n, index):
        block = kbuf.at[0, 0:2] if n == 1 else kbuf.at[0:2]
        remote(block, block, kv, 1, index, sib).wait_recv()

    def o_up(s, h):
        return remote(osnd.at[s, h], orcv.at[s, h], (left, or_), 3, (s, h), y_up)

    def o_dn(s, h):
        return remote(
            osnd.at[yh + s, h], orcv.at[yh + s, h], (left, or_), 3, (yh + s, h), y_dn
        )

    def z_upc(s, n):
        return remote(zsnd.at[s, n], zrcv.at[s, n], (left, zr), 4, (s, n), z_up)

    def z_dnc(s, n):
        place = nz - 2 - s
        return remote(zsnd.at[place, n], zrcv.at[place, n], (left, zr), 4, (place, n), z_dn)

    loads[0].wait()
    alive = (mask_ref[...] == 0).astype(f32)
    alive8 = jnp.broadcast_to(alive, (8, count))
    before = (
        lax.broadcasted_iota(jnp.int32, (count, count), 0)
        < lax.broadcasted_iota(jnp.int32, (count, count), 1)
    ).astype(f32)
    rank = dot(alive8.astype(bf16), before.astype(bf16))[0:1]
    slot = lax.broadcasted_iota(jnp.int32, (live, count), 0).astype(f32)
    picks = jnp.where((slot == rank) & (alive > 0.5), 1.0, 0.0)
    sel_ref[...] = picks.T.astype(bf16)
    picks = picks.astype(bf16)

    def normed_head(ref, gain_ref, h):
        part = ref[:, h * depth : (h + 1) * depth].astype(f32)
        square = jnp.mean(part * part, axis=-1, keepdims=True)
        return part * lax.rsqrt(square + 1e-06) * gain_ref[...]

    for load in loads[1:3]:
        load.wait()
    for h in range(heads):
        qn = normed_head(q_ref, qg_ref, h).astype(bf16)
        qbuf[0, h] = dot(picks, qn).T.astype(bf16)
        if h == 0:
            pl.semaphore_wait(barrier, 8)
        q_up(0, h).start()
        q_dn(0, h).start()
    for load in loads[3:6]:
        load.wait()
    for h in range(heads):
        kbuf[0, h] = normed_head(k_ref, kg_ref, h).astype(bf16)
        k_out(h).start()
        vbuf[0, h] = v_ref[:, h * depth : (h + 1) * depth].astype(f32).T.astype(bf16)
        v_out(h).start()
        k_sib(h).start()
        v_sib(h).start()

    def lanes(ref, a, b, *index):
        return jnp.concatenate([ref[(a, *index)], ref[(b, *index)]], axis=1)

    def halves(a, b, first):
        pair = (0, 1) if first else (2, 3)

        def scores_of(h):
            q2 = lanes(qbuf, a, b, h)
            return [dot(kbuf[j, h], q2) for j in pair]

        ahead = scores_of(0)
        for h in range(heads):
            scores = ahead
            if h + 1 < heads:
                ahead = scores_of(h + 1)
            top = jnp.maximum(*[jnp.max(s, axis=0, keepdims=True) for s in scores])
            top = top.astype(bf16).astype(f32)
            if not first:
                old = lanes(stat, a, b, h, slice(0, 1))
                top = jnp.maximum(top, old)
            weights = [jnp.exp2((s - top) * c2) for s in scores]
            total = sum(jnp.sum(w, axis=0, keepdims=True) for w in weights)
            summed = sum(dot(vbuf[j, h], w.astype(bf16)) for j, w in zip(pair, weights))
            if not first:
                factor = jnp.exp2((old - top) * c2)
                total += factor * lanes(stat, a, b, h, slice(1, 2))
                summed += factor * lanes(oacc, a, b, h)
            yield summed, top, total

    def near(a, b):
        for h, (summed, top, total) in enumerate(halves(a, b, True)):
            for n, place in enumerate((a, b)):
                part = slice(n * live, (n + 1) * live)
                oacc[place, h] = summed[:, part]
                stat[place, h, 0:1] = top[:, part]
                stat[place, h, 1:2] = total[:, part]

    def relay(g):
        kv_come(1, first_leg + g)
        k_on(g).start()
        v_on(g).start()

    def last_leg(g):
        kv_come(1, second_leg + g)
        k_last(g).start()
        v_last(g).start()

    def q_pass(s):
        for h in range(heads):
            q_up(s, h).wait_recv()
            q_up(s + 1, h).start()
            q_dn(s, h).wait_recv()

            @pl.when(s < yh - 2)
            def _():
                q_dn(s + 1, h).start()

    def q_step(s, carry):
        @pl.when(s == 1)
        def _():
            relay(1)

        q_pass(s)

        @pl.when(s == 0)
        def _():
            kv_come(heads, 0)
            relay(0)

        @pl.when(s == 1)
        def _():
            relay(2)

        @pl.when(s == 2)
        def _():
            last_leg(0)
            last_leg(1)

        near(ny - 1 - s, s + 1)
        return carry

    lax.fori_loop(0, yh - 1, q_step, 0)
    last_leg(2)
    for h in range(heads):
        q_up(yh - 1, h).wait_recv()
    near(yh, 0)
    kv_come(heads, 1)

    def put(way, s, h, summed, top, total):
        osnd[way * yh + s, h, 0:depth] = summed.astype(bf16)
        high = total.astype(bf16).astype(f32)
        row = lax.broadcasted_iota(jnp.int32, (16, live), 0)
        tile = jnp.where(row == 0, top, jnp.where(row == 1, high, total - high))
        osnd[way * yh + s, h, depth : depth + 16] = tile.astype(bf16)

    def merge(way, s, h, summed, top, total):
        theirs = orcv[way * yh + s, h, 0:depth].astype(f32)
        tile = orcv[way * yh + s, h, depth : depth + 16].astype(f32)
        their_top, their_total = tile[0:1], tile[1:2] + tile[2:3]
        newest = jnp.maximum(top, their_top)
        mine, factor = jnp.exp2((top - newest) * c2), jnp.exp2((their_top - newest) * c2)
        return summed * mine + theirs * factor, newest, total * mine + their_total * factor

    def split(parts, n):
        return [part[:, n * live : (n + 1) * live] for part in parts]

    for h, parts in enumerate(halves(yh, yh + 1, False)):
        put(0, 0, h, *split(parts, 0))
        o_up(0, h).start()
        put(1, 0, h, *split(parts, 1))
        o_dn(0, h).start()

    def o_step(s, carry):
        for h, (summed, top, total) in enumerate(halves(yh - s, lax.rem(yh + 1 + s, ny), False)):
            part_o[h] = summed
            part_s[h, 0:1] = top
            part_s[h, 1:2] = total
        for h in range(heads):
            parts = (part_o[h], part_s[h, 0:1], part_s[h, 1:2])
            o_up(s - 1, h).wait_recv()
            put(0, s, h, *merge(0, s - 1, h, *split(parts, 0)))
            o_up(s, h).start()
            o_dn(s - 1, h).wait_recv()
            summed, top, total = merge(1, s - 1, h, *split(parts, 1))
            put(1, s, h, summed, top, total)

            @pl.when(s < yh - 1)
            def _():
                o_dn(s, h).start()

            own_o[h] = summed
            own_s[h, 0:1] = top
            own_s[h, 1:2] = total
        return carry

    lax.fori_loop(1, yh, o_step, 0)

    for h in range(heads):
        o_up(yh - 1, h).wait_recv()
        summed, top, total = merge(0, yh - 1, h, own_o[h], own_s[h, 0:1], own_s[h, 1:2])
        done = (summed / total).astype(bf16)
        att_ref[:, h * depth : (h + 1) * depth] = dot(sel_ref[...], done, (1, 1)).astype(bf16)

    loads[6].wait()

    def rows_of(n, place):
        start = pl.multiple_of(place * share, share)
        return pbuf[n, pl.ds(start, share), :]

    def hops(n):
        odd = lax.rem(n, 2)
        return zh - odd, zh - 1 + odd

    def z_first(n, carry):
        up, down = hops(n)
        columns = pl.ds(pl.multiple_of(n * cut, cut), cut)
        pbuf[n] = dot(att_ref[...], w_ref[:, columns])
        zsnd[0, n] = rows_of(n, lax.rem(tp + up, nz)).astype(bf16)
        z_upc(0, n).start()
        zsnd[nz - 2, n] = rows_of(n, lax.rem(tp + nz - down, nz)).astype(bf16)
        z_dnc(0, n).start()
        return carry

    lax.fori_loop(0, cuts, z_first, 0)

    def z_step(s, carry):
        def z_cut(n, inner):
            up, down = hops(n)

            @pl.when(s < up)
            def _():
                z_upc(s - 1, n).wait_recv()
                part = rows_of(n, lax.rem(tp + up - s, nz))
                zsnd[s, n] = (part + zrcv[s - 1, n].astype(f32)).astype(bf16)
                z_upc(s, n).start()

            @pl.when(s < down)
            def _():
                z_dnc(s - 1, n).wait_recv()
                part = rows_of(n, lax.rem(tp + nz - down + s, nz))
                zsnd[nz - 2 - s, n] = (part + zrcv[nz - 1 - s, n].astype(f32)).astype(bf16)
                z_dnc(s, n).start()

            return inner

        return lax.fori_loop(0, cuts, z_cut, carry)

    lax.fori_loop(1, zh, z_step, 0)

    for load in loads[7:]:
        load.wait()
    own_rows = pl.ds(pl.multiple_of(tp * share, share), share)
    alive_rows = jnp.sum(sel_ref[own_rows, :].astype(f32), axis=1, keepdims=True) > 0.5
    sums = jnp.zeros((share, 1), f32)
    for n in range(cuts):
        columns = slice(n * cut, (n + 1) * cut)
        up, down = zh - n % 2, zh - 1 + n % 2
        z_upc(up - 1, n).wait_recv()
        z_dnc(down - 1, n).wait_recv()
        projected = (
            rows_of(n, tp) + zrcv[up - 1, n].astype(f32) + zrcv[nz - 1 - down, n].astype(f32)
        )
        mixed = bi_ref[:, columns].astype(f32) + gate_ref[:, columns] * projected
        out = jnp.where(alive_rows, mixed, co_ref[:, columns].astype(f32)).astype(bf16)
        bo_ref[:, columns] = out
        sums += jnp.sum(out.astype(f32), axis=1, keepdims=True)
    store = pltpu.make_async_copy(bo_ref, bo_out, loc_sem.at[13])
    store.start()
    center = sums * (1.0 / feats)
    away = bo_ref[...].astype(f32) - center
    spread = jnp.mean(away * away, axis=1, keepdims=True)
    normed = away * lax.rsqrt(spread + 1e-06) * (1.0 + scale_ref[...]) + shift_ref[...]
    ysnd[...] = dot(normed.astype(bf16), pw_ref[...], (1, 1))
    swap = remote(ysnd, yrcv, (left, yr), 5, 0, other)
    swap.start()

    for kind, sent in enumerate(
        (qbuf.at[0 : ny - 1], kbuf, vbuf, osnd.at[0 : ny - 1], zsnd)
    ):
        remote(sent, sent, (left, qr), kind, (0, 0), sib).wait_send()
    swap.wait()
    mine, theirs = ysnd[...], yrcv[...]
    cond = jnp.where(cfg == 0, mine, theirs)
    uncond = jnp.where(cfg == 0, theirs, mine)
    velocity = uncond + guidance_scale * (cond - uncond)
    half_width = vel_ref.shape[1]
    vel_ref[...] = jnp.where(cfg == 0, velocity[:, :half_width], velocity[:, half_width:])
    last = pltpu.make_async_copy(vel_ref, vel_out, loc_sem.at[14])
    last.start()
    store.wait()
    last.wait()


def shards(
    query_proj,
    key_proj,
    value_proj,
    query_gain,
    key_gain,
    block_input,
    cached_out,
    replay_mask,
    branch_gate,
    attn_weight,
    final_shift,
    final_scale,
    patch_weight,
):
    ny = lax.axis_size("ctx") // 4
    nz = lax.axis_size("tp")
    count, width = query_proj.shape[1:]
    depth = query_gain.shape[0]
    heads = width // depth
    live = count // 2
    share, feats = block_input.shape[1:]
    channels = patch_weight.shape[1]
    yh, zh = ny // 2, nz // 2
    cuts = feats // cut
    anywhere = pl.BlockSpec(memory_space=pl.ANY)
    hbm = pl.BlockSpec(memory_space=pltpu.HBM)
    dma = pltpu.SemaphoreType.DMA
    operands = (
        query_proj[0],
        key_proj[0],
        value_proj[0],
        query_gain[None],
        key_gain[None],
        replay_mask,
        branch_gate,
        final_shift,
        final_scale,
        block_input[0],
        cached_out[0],
        attn_weight,
        patch_weight.T,
    )
    block_out, velocity = pl.pallas_call(
        functools.partial(kernel, ny, nz),
        out_shape=(
            jax.ShapeDtypeStruct((share, feats), bf16),
            jax.ShapeDtypeStruct((share, channels // 2), f32),
        ),
        in_specs=[hbm] * 13,
        out_specs=(anywhere, anywhere),
        scratch_shapes=[
            pltpu.VMEM((share, feats), bf16),
            pltpu.VMEM((share, channels // 2), f32),
            *[pltpu.VMEM((count, width), bf16)] * 3,
            *[pltpu.VMEM((1, depth), f32)] * 2,
            pltpu.VMEM((1, count), jnp.int32),
            *[pltpu.VMEM((1, feats), f32)] * 3,
            *[pltpu.VMEM((share, feats), bf16)] * 2,
            pltpu.VMEM((width, feats), bf16),
            pltpu.VMEM((channels, feats), bf16),
            pltpu.VMEM((count, live), bf16),
            pltpu.VMEM((4, heads, count, depth), bf16),
            pltpu.VMEM((4, heads, depth, count), bf16),
            pltpu.VMEM((heads, count, depth), bf16),
            pltpu.VMEM((heads, depth, count), bf16),
            pltpu.VMEM((ny, heads, depth, live), bf16),
            pltpu.VMEM((ny, heads, depth, live), f32),
            pltpu.VMEM((ny, heads, 8, live), f32),
            pltpu.VMEM((heads, depth, 2 * live), f32),
            pltpu.VMEM((heads, 8, 2 * live), f32),
            pltpu.VMEM((heads, depth, live), f32),
            pltpu.VMEM((heads, 8, live), f32),
            *[pltpu.VMEM((ny, heads, depth + 16, live), bf16)] * 2,
            pltpu.VMEM((count, width), bf16),
            pltpu.VMEM((cuts, count, cut), f32),
            *[pltpu.VMEM((nz - 1, cuts, share, cut), bf16)] * 2,
            pltpu.VMEM((share, channels), f32),
            pltpu.VMEM((share, channels), f32),
            dma((15,)),
            dma((6,)),
            dma((ny - 1, heads)),
            dma((3 * heads,)),
            dma((ny - 1, heads)),
            dma((nz - 1, cuts)),
            dma((1,)),
        ],
        compiler_params=pltpu.CompilerParams(
            collective_id=0, has_side_effects=True, vmem_limit_bytes=32 * 1024 * 1024
        ),
        name="block",
    )(*[pltpu.with_memory_space_constraint(operand, pltpu.HBM) for operand in operands])
    return (block_out[None], velocity)


def solution(mesh):
    in_specs = (
        P("cfg", "ctx", "tp"),
        P("cfg", "ctx", "tp"),
        P("cfg", "ctx", "tp"),
        P(),
        P(),
        P("cfg", ("ctx", "tp"), None),
        P("cfg", ("ctx", "tp"), None),
        P("cfg", "ctx"),
        P("cfg", None),
        P("tp", None),
        P("cfg", None),
        P("cfg", None),
        P(),
    )
    out_specs = (P("cfg", ("ctx", "tp"), None), P(("ctx", "tp"), "cfg"))
    return jax.shard_map(shards, mesh=mesh, in_specs=in_specs, out_specs=out_specs, check_vma=False)
```

time: 74.2 us -> 66.9 us (0.902)
  the two profiles are of different devices: /device:TPU:2 before, /device:TPU:4 now
where the time goes in v2:
time: 66.9 us; the launch traced here: 66.8 us
  Pallas kernels  64.9 us (97%)
  local copies, waits for them, and re-layouts  1.28 us (2%)
    pallas_call x1, Pallas kernels, shards(): pl.pallas_call(functools.partial(kernel, ny, nz), out_shape=(jax.ShapeDty...  64.9 us

profile of v2, /device:TPU:4, one launch (start us, length us, event | category | flops | bytes accessed | tf_op | source)
XLA Modules:
  0.0 66.8 jit_solution(17229337916049267100)
XLA Ops:
  0.6 64.9 %block.1 = (bf16[32,3072]{1,0:T(8,128)(2,1)S(1)}, f32[32,32]{1,0:T(8,128)S(1)}) custom-call(bf16[256,384]{1,0:T(8,128)(2,1)} %bitcast.11, bf16[256,384]{1,0:T(8,128)(2,1)} %bitcast.12, bf16[256,384]{1,0:T(8,128)(2,1)} %bitcast.13, f32[1,128]{1,0:T(1,128)} %bitcast.16, f32[1,128]{1,0:T(1,128)} %bitcast.17, s32[1,256]{1,0:T(1,128)} %mask_hbm.1, ...), custom_call_target="tpu_custom_call" | custom-call | tf_op jit(solution)/shard_map/block/pallas_call | solution.py:517
  65.5 0.7 %copy.17 = bf16[1,32,3072]{2,1,0:T(8,128)(2,1)} copy(bf16[1,32,3072]{2,1,0:T(8,128)(2,1)S(1)} %bitcast.9) | data formatting | bytes 393216
  66.2 0.6 copy.18

commit v3 on v2

--- a/solution.py
+++ b/solution.py
@@ -156,7 +156,7 @@
         return remote(qbuf.at[s, h], qbuf.at[s + 1, h], (left, qr), 0, (yh + s, h), y_dn)
 
     kv = (left, kr)
-    first_leg, second_leg = heads, 2 * heads
+    first_leg, second_leg, third_leg = 1, 1 + heads, 1 + 2 * heads
 
     def k_sib(h):
         return remote(kbuf.at[0, h], kbuf.at[1, h], kv, 1, 0, sib)
@@ -177,10 +177,10 @@
         return remote(rv.at[h], vbuf.at[2, h], kv, 2, second_leg + h, x_dn)
 
     def k_last(h):
-        return remote(kbuf.at[2, h], kbuf.at[3, h], kv, 1, 1, sib)
+        return remote(kbuf.at[2, h], kbuf.at[3, h], kv, 1, third_leg + h, sib)
 
     def v_last(h):
-        return remote(vbuf.at[2, h], vbuf.at[3, h], kv, 2, 1, sib)
+        return remote(vbuf.at[2, h], vbuf.at[3, h], kv, 2, third_leg + h, sib)
 
     def kv_come(n, index):
         block = kbuf.at[0, 0:2] if n == 1 else kbuf.at[0:2]
@@ -224,52 +224,55 @@
     for h in range(heads):
         qn = normed_head(q_ref, qg_ref, h).astype(bf16)
         qbuf[0, h] = dot(picks, qn).T.astype(bf16)
-        if h == 0:
-            pl.semaphore_wait(barrier, 8)
+    pl.semaphore_wait(barrier, 8)
+    for h in range(heads):
         q_up(0, h).start()
         q_dn(0, h).start()
     for load in loads[3:6]:
         load.wait()
     for h in range(heads):
         kbuf[0, h] = normed_head(k_ref, kg_ref, h).astype(bf16)
+        vbuf[0, h] = v_ref[:, h * depth : (h + 1) * depth].astype(f32).T.astype(bf16)
+    for h in range(heads):
         k_out(h).start()
-        vbuf[0, h] = v_ref[:, h * depth : (h + 1) * depth].astype(f32).T.astype(bf16)
         v_out(h).start()
         k_sib(h).start()
         v_sib(h).start()
 
-    def lanes(ref, a, b, *index):
-        return jnp.concatenate([ref[(a, *index)], ref[(b, *index)]], axis=1)
-
-    def halves(a, b, first):
-        pair = (0, 1) if first else (2, 3)
-
+    def lanes(ref, places, *index):
+        parts = [ref[(place, *index)] for place in places]
+        return parts[0] if len(parts) == 1 else jnp.concatenate(parts, axis=1)
+
+    def sums(places, slots, stored, which=range(heads)):
         def scores_of(h):
-            q2 = lanes(qbuf, a, b, h)
-            return [dot(kbuf[j, h], q2) for j in pair]
-
-        ahead = scores_of(0)
-        for h in range(heads):
+            queries = lanes(qbuf, places, h)
+            return [dot(kbuf[j, h], queries) for j in slots]
+
+        which = list(which)
+        ahead = scores_of(which[0])
+        for n, h in enumerate(which):
             scores = ahead
-            if h + 1 < heads:
-                ahead = scores_of(h + 1)
-            top = jnp.maximum(*[jnp.max(s, axis=0, keepdims=True) for s in scores])
+            if n + 1 < len(which):
+                ahead = scores_of(which[n + 1])
+            top = functools.reduce(
+                jnp.maximum, [jnp.max(s, axis=0, keepdims=True) for s in scores]
+            )
             top = top.astype(bf16).astype(f32)
-            if not first:
-                old = lanes(stat, a, b, h, slice(0, 1))
+            if stored:
+                old = lanes(stat, places, h, slice(0, 1))
                 top = jnp.maximum(top, old)
             weights = [jnp.exp2((s - top) * c2) for s in scores]
             total = sum(jnp.sum(w, axis=0, keepdims=True) for w in weights)
-            summed = sum(dot(vbuf[j, h], w.astype(bf16)) for j, w in zip(pair, weights))
-            if not first:
+            summed = sum(dot(vbuf[j, h], w.astype(bf16)) for j, w in zip(slots, weights))
+            if stored:
                 factor = jnp.exp2((old - top) * c2)
-                total += factor * lanes(stat, a, b, h, slice(1, 2))
-                summed += factor * lanes(oacc, a, b, h)
+                total += factor * lanes(stat, places, h, slice(1, 2))
+                summed += factor * lanes(oacc, places, h)
             yield summed, top, total
 
-    def near(a, b):
-        for h, (summed, top, total) in enumerate(halves(a, b, True)):
-            for n, place in enumerate((a, b)):
+    def near(*places):
+        for h, (summed, top, total) in enumerate(sums(places, (0, 1), False)):
+            for n, place in enumerate(places):
                 part = slice(n * live, (n + 1) * live)
                 oacc[place, h] = summed[:, part]
                 stat[place, h, 0:1] = top[:, part]
@@ -295,6 +298,15 @@
             def _():
                 q_dn(s + 1, h).start()
 
+            if h < heads - 1:
+
+                @pl.when(s == yh - 2)
+                def _():
+                    last_leg(h)
+
+    kv_come(heads, 0)
+    near(0)
+
     def q_step(s, carry):
         @pl.when(s == 1)
         def _():
@@ -304,27 +316,17 @@
 
         @pl.when(s == 0)
         def _():
-            kv_come(heads, 0)
             relay(0)
 
         @pl.when(s == 1)
         def _():
             relay(2)
 
-        @pl.when(s == 2)
-        def _():
-            last_leg(0)
-            last_leg(1)
-
         near(ny - 1 - s, s + 1)
         return carry
 
     lax.fori_loop(0, yh - 1, q_step, 0)
     last_leg(2)
-    for h in range(heads):
-        q_up(yh - 1, h).wait_recv()
-    near(yh, 0)
-    kv_come(heads, 1)
 
     def put(way, s, h, summed, top, total):
         osnd[way * yh + s, h, 0:depth] = summed.astype(bf16)
@@ -341,36 +343,50 @@
         mine, factor = jnp.exp2((top - newest) * c2), jnp.exp2((their_top - newest) * c2)
         return summed * mine + theirs * factor, newest, total * mine + their_total * factor
 
-    def split(parts, n):
-        return [part[:, n * live : (n + 1) * live] for part in parts]
-
-    for h, parts in enumerate(halves(yh, yh + 1, False)):
-        put(0, 0, h, *split(parts, 0))
-        o_up(0, h).start()
-        put(1, 0, h, *split(parts, 1))
+    for h in range(heads):
+        q_up(yh - 1, h).wait_recv()
+        kv_come(1, third_leg + h)
+        for parts in sums((yh,), range(4), False, (h,)):
+            put(0, 0, h, *parts)
+            o_up(0, h).start()
+    for h, parts in enumerate(sums((yh + 1,), (2, 3), True)):
+        put(1, 0, h, *parts)
         o_dn(0, h).start()
 
+    def own_sums(s):
+        places = (yh - s, lax.rem(yh + 1 + s, ny))
+        for h, (summed, top, total) in enumerate(sums(places, (2, 3), True)):
+            part_o[lax.rem(s, 2), h] = summed
+            part_s[lax.rem(s, 2), h, 0:1] = top
+            part_s[lax.rem(s, 2), h, 1:2] = total
+
+    def own_part(s, h, way):
+        side = slice(way * live, (way + 1) * live)
+        step = lax.rem(s, 2)
+        return part_o[step, h, :, side], part_s[step, h, 0:1, side], part_s[step, h, 1:2, side]
+
+    own_sums(1)
+
     def o_step(s, carry):
-        for h, (summed, top, total) in enumerate(halves(yh - s, lax.rem(yh + 1 + s, ny), False)):
-            part_o[h] = summed
-            part_s[h, 0:1] = top
-            part_s[h, 1:2] = total
         for h in range(heads):
-            parts = (part_o[h], part_s[h, 0:1], part_s[h, 1:2])
             o_up(s - 1, h).wait_recv()
-            put(0, s, h, *merge(0, s - 1, h, *split(parts, 0)))
+            put(0, s, h, *merge(0, s - 1, h, *own_part(s, h, 0)))
             o_up(s, h).start()
+
+        @pl.when(s < yh - 1)
+        def _():
+            own_sums(s + 1)
+
+        for h in range(heads):
             o_dn(s - 1, h).wait_recv()
-            summed, top, total = merge(1, s - 1, h, *split(parts, 1))
-            put(1, s, h, summed, top, total)
+            below = merge(1, s - 1, h, *own_part(s, h, 1))
 
             @pl.when(s < yh - 1)
             def _():
+                put(1, s, h, *below)
                 o_dn(s, h).start()
 
-            own_o[h] = summed
-            own_s[h, 0:1] = top
-            own_s[h, 1:2] = total
+            own_o[h], own_s[h, 0:1], own_s[h, 1:2] = below
         return carry
 
     lax.fori_loop(1, yh, o_step, 0)
@@ -403,29 +419,35 @@
 
     lax.fori_loop(0, cuts, z_first, 0)
 
+    def passed(place, n, dest):
+        return rows_of(n, dest) + zrcv[place, n].astype(f32)
+
     def z_step(s, carry):
         def z_cut(n, inner):
             up, down = hops(n)
-
-            @pl.when(s < up)
-            def _():
-                z_upc(s - 1, n).wait_recv()
-                part = rows_of(n, lax.rem(tp + up - s, nz))
-                zsnd[s, n] = (part + zrcv[s - 1, n].astype(f32)).astype(bf16)
-                z_upc(s, n).start()
-
-            @pl.when(s < down)
-            def _():
-                z_dnc(s - 1, n).wait_recv()
-                part = rows_of(n, lax.rem(tp + nz - down + s, nz))
-                zsnd[nz - 2 - s, n] = (part + zrcv[nz - 1 - s, n].astype(f32)).astype(bf16)
-                z_dnc(s, n).start()
-
+            z_upc(s - 1, n).wait_recv()
+            z_dnc(s - 1, n).wait_recv()
+            above = passed(s - 1, n, lax.rem(tp + up - s, nz))
+            below = passed(nz - 1 - s, n, lax.rem(tp + nz - down + s, nz))
+            zsnd[s, n] = above.astype(bf16)
+            zsnd[nz - 2 - s, n] = below.astype(bf16)
+            z_upc(s, n).start()
+            z_dnc(s, n).start()
             return inner
 
         return lax.fori_loop(0, cuts, z_cut, carry)
 
-    lax.fori_loop(1, zh, z_step, 0)
+    lax.fori_loop(1, zh - 1, z_step, 0)
+
+    for n in range(cuts):
+        if n % 2 == 0:
+            z_upc(zh - 2, n).wait_recv()
+            zsnd[zh - 1, n] = passed(zh - 2, n, lax.rem(tp + 1, nz)).astype(bf16)
+            z_upc(zh - 1, n).start()
+        else:
+            z_dnc(zh - 2, n).wait_recv()
+            zsnd[zh - 1, n] = passed(zh, n, lax.rem(tp + nz - 1, nz)).astype(bf16)
+            z_dnc(zh - 1, n).start()
 
     for load in loads[7:]:
         load.wait()
@@ -455,7 +477,7 @@
     swap.start()
 
     for kind, sent in enumerate(
-        (qbuf.at[0 : ny - 1], kbuf, vbuf, osnd.at[0 : ny - 1], zsnd)
+        (qbuf.at[0 : ny - 1], kbuf, vbuf, osnd, zsnd)
     ):
         remote(sent, sent, (left, qr), kind, (0, 0), sib).wait_send()
     swap.wait()
@@ -540,11 +562,11 @@
             pltpu.VMEM((ny, heads, depth, live), bf16),
             pltpu.VMEM((ny, heads, depth, live), f32),
             pltpu.VMEM((ny, heads, 8, live), f32),
-            pltpu.VMEM((heads, depth, 2 * live), f32),
-            pltpu.VMEM((heads, 8, 2 * live), f32),
+            pltpu.VMEM((2, heads, depth, 2 * live), f32),
+            pltpu.VMEM((2, heads, 8, 2 * live), f32),
             pltpu.VMEM((heads, depth, live), f32),
             pltpu.VMEM((heads, 8, live), f32),
-            *[pltpu.VMEM((ny, heads, depth + 16, live), bf16)] * 2,
+            *[pltpu.VMEM((ny - 1, heads, depth + 16, live), bf16)] * 2,
             pltpu.VMEM((count, width), bf16),
             pltpu.VMEM((cuts, count, cut), f32),
             *[pltpu.VMEM((nz - 1, cuts, share, cut), bf16)] * 2,
@@ -553,7 +575,7 @@
             dma((15,)),
             dma((6,)),
             dma((ny - 1, heads)),
-            dma((3 * heads,)),
+            dma((1 + 3 * heads,)),
             dma((ny - 1, heads)),
             dma((nz - 1, cuts)),
             dma((1,)),

time: 66.9 us -> 65.4 us (0.978)
  Pallas kernels: 64.9 us -> 63.3 us
    pallas_call x1, Pallas kernels: 64.9 us -> 63.3 us  [shards(): pl.pallas_call(functools.partial(kernel, ny, nz), out_shape=(jax.ShapeDty...]
where the time goes in v3:
time: 65.4 us; the launch traced here: 65.2 us
  Pallas kernels  63.3 us (97%)
  local copies, waits for them, and re-layouts  1.28 us (2%)
    pallas_call x1, Pallas kernels, shards(): pl.pallas_call(functools.partial(kernel, ny, nz), out_shape=(jax.ShapeDty...  63.3 us

profile of v3, /device:TPU:4, one launch (start us, length us, event | category | flops | bytes accessed | tf_op | source)
XLA Modules:
  0.0 65.2 jit_solution(767941051940025025)
XLA Ops:
  0.6 63.3 %block.1 = (bf16[32,3072]{1,0:T(8,128)(2,1)S(1)}, f32[32,32]{1,0:T(8,128)S(1)}) custom-call(bf16[256,384]{1,0:T(8,128)(2,1)} %bitcast.11, bf16[256,384]{1,0:T(8,128)(2,1)} %bitcast.12, bf16[256,384]{1,0:T(8,128)(2,1)} %bitcast.13, f32[1,128]{1,0:T(1,128)} %bitcast.16, f32[1,128]{1,0:T(1,128)} %bitcast.17, s32[1,256]{1,0:T(1,128)} %mask_hbm.1, ...), custom_call_target="tpu_custom_call" | custom-call | tf_op jit(solution)/shard_map/block/pallas_call | solution.py:539
  64.0 0.7 %copy.17 = bf16[1,32,3072]{2,1,0:T(8,128)(2,1)} copy(bf16[1,32,3072]{2,1,0:T(8,128)(2,1)S(1)} %bitcast.9) | data formatting | bytes 393216
  64.6 0.6 copy.18

commit v4 on v3

--- a/solution.py
+++ b/solution.py
@@ -491,6 +491,17 @@
     last.start()
     store.wait()
     last.wait()
+
+
+def hand_over(a_ref, b_ref, a_out, b_out, sems):
+    copies = (
+        pltpu.make_async_copy(a_ref, a_out, sems.at[0]),
+        pltpu.make_async_copy(b_ref, b_out, sems.at[1]),
+    )
+    for copy in copies:
+        copy.start()
+    for copy in copies:
+        copy.wait()
 
 
 def shards(
@@ -585,6 +596,18 @@
         ),
         name="block",
     )(*[pltpu.with_memory_space_constraint(operand, pltpu.HBM) for operand in operands])
+    vmem = pl.BlockSpec(memory_space=pl.ANY)
+    block_out, velocity = pl.pallas_call(
+        hand_over,
+        out_shape=(
+            jax.ShapeDtypeStruct(block_out.shape, bf16),
+            jax.ShapeDtypeStruct(velocity.shape, f32),
+        ),
+        in_specs=[vmem] * 2,
+        out_specs=(hbm, hbm),
+        scratch_shapes=[dma((2,))],
+        name="hand_over",
+    )(*[pltpu.with_memory_space_constraint(part, pltpu.VMEM) for part in (block_out, velocity)])
     return (block_out[None], velocity)
 
 

time: 65.4 us -> 64.8 us (level)
  local copies, waits for them, and re-layouts: 1.28 us -> 0 us
  Pallas kernels: 63.3 us -> 64 us
    unnamed x2 -> x0, local copies, waits for them, and re-layouts: 1.28 us -> none
    pallas_call x0 -> x1, Pallas kernels: none -> 0.7 us  [shards(): pl.pallas_call(hand_over, out_shape=(jax.ShapeDtypeStruct(block_out.shape...]
where the time goes in v4:
time: 64.8 us; the launch traced here: 64.7 us
  Pallas kernels  64 us (99%)
    pallas_call x1, Pallas kernels, shards(): pl.pallas_call(functools.partial(kernel, ny, nz), out_shape=(jax.ShapeDty...  63.3 us

profile of v4, /device:TPU:4, one launch (start us, length us, event | category | flops | bytes accessed | tf_op | source)
XLA Modules:
  0.0 64.7 jit_solution(16227465024803070067)
XLA Ops:
  0.6 63.3 %block.1 = (bf16[32,3072]{1,0:T(8,128)(2,1)S(1)}, f32[32,32]{1,0:T(8,128)S(1)}) custom-call(bf16[256,384]{1,0:T(8,128)(2,1)} %bitcast.10, bf16[256,384]{1,0:T(8,128)(2,1)} %bitcast.11, bf16[256,384]{1,0:T(8,128)(2,1)} %bitcast.12, f32[1,128]{1,0:T(1,128)} %bitcast.15, f32[1,128]{1,0:T(1,128)} %bitcast.16, s32[1,256]{1,0:T(1,128)} %mask_hbm.1, ...), custom_call_target="tpu_custom_call" | custom-call | tf_op jit(solution)/shard_map/block/pallas_call | solution.py:550
  64.0 0.7 %hand_over.1 = (bf16[32,3072]{1,0:T(8,128)(2,1)}, f32[32,32]{1,0:T(8,128)}) custom-call(bf16[32,3072]{1,0:T(8,128)(2,1)S(1)} %get-tuple-element.6.a_ref, f32[32,32]{1,0:T(8,128)S(1)} %get-tuple-element.7.b_ref), custom_call_target="tpu_custom_call" | custom-call | tf_op jit(solution)/shard_map/hand_over/pallas_call | solution.py:600
